TPU v7x, 512 devices: a whole 4x8x8 slice. The times are simulated.
512 devices in a mesh: fsdp: 64 (over x, y, core), dp: 8 (over z).
Axes of the slice: x: 4, y: 8, z: 8, core: 2. Of those that a mesh axis runs over, the one named last changes fastest.
Arguments:
- grads: bfloat16 [8, 1024, 28672], P('dp', 'fsdp')
- block_slot: int32 [28], replicated, may hold values from 0 to 63, as said below
- left_stats: float32 [64, 1024, 1024], P('fsdp', 'dp')
- right_stats: float32 [64, 1024, 1024], P('fsdp', 'dp')
- left_root: bfloat16 [64, 1024, 1024], P('fsdp', 'dp')
- right_root: bfloat16 [64, 1024, 1024], P('fsdp', 'dp')
Outputs:
- left_new: float32 [64, 1024, 1024], P('fsdp', 'dp')
- right_new: float32 [64, 1024, 1024], P('fsdp', 'dp')
- update: bfloat16 [1024, 28672], P('fsdp')
Inputs may be any that keep to these rules, and one draw needn't show every extreme that they name: The entries of block_slot are distinct. Block b's statistics and roots sit in slot block_slot[b], which belongs to the fsdp device of index block_slot[b]; slots that no block names are empty and their statistics pass through unchanged.
All inputs are finite; a program needn't handle non-finite values.
Results may differ from a plain program's by a relative error of at most 0.015.
Values may be sent and summed in bfloat16 or wider, within the bound.
No kernel may reach another device: no remote copies, remote signals or barrier semaphores. Data moves between devices by JAX's collectives and lax.ppermute only.
A program may use at most 64 MiB of HBM per device.

v0:
```python
import jax
import jax.numpy as jnp
from jax import lax
from jax.sharding import Mesh
from jax.sharding import PartitionSpec as P

FSDP = ("fsdp_0", "fsdp_1", "fsdp_2")
epsilon = 1e-06


def split_terms(value):
    high = lax.reduce_precision(value, 8, 7)
    middle = lax.reduce_precision(value - high, 8, 7)
    low = value - high - middle
    return [term.astype(jnp.bfloat16) for term in (high, middle, low)]


def per_device(grads, block_slot, left_stats, right_stats, left_root, right_root):
    rows = grads[0]
    row_dev, col_count = rows.shape
    block_size = left_stats.shape[2]
    block_count = col_count // block_size
    shared = left_stats.shape[1]
    replicas = lax.axis_size("dp")
    total_slots = lax.axis_size(FSDP)
    slot_ids = jnp.arange(total_slots, dtype=jnp.int32)
    matches = block_slot[None, :] == slot_ids[:, None]
    filled = jnp.any(matches, axis=1)
    numbers = jnp.arange(block_count, dtype=jnp.int32)
    source = jnp.sum(jnp.where(matches, numbers[None, :], 0), axis=1)
    whole_left = lax.all_gather(left_root[0], "dp", axis=0, tiled=True)
    shares = rows.reshape(row_dev, block_count, replicas, shared).transpose(2, 1, 0, 3)
    shares = shares.reshape(replicas, block_count * row_dev, shared)
    roots = right_root[0].reshape(shared, replicas, shared).transpose(1, 0, 2)
    message = jnp.concatenate([shares, roots], axis=1)
    received = lax.all_to_all(message, "dp", 0, 0, tiled=True)
    summed = jnp.sum(received[:, : block_count * row_dev].astype(jnp.float32), axis=0)
    summed = summed.astype(jnp.bfloat16).reshape(block_count, row_dev, shared)
    right_cols = received[:, block_count * row_dev :]
    outgoing = jnp.where(
        filled[:, None, None], jnp.take(summed, source, axis=0), jnp.zeros((), jnp.bfloat16)
    )
    incoming = lax.all_to_all(outgoing, FSDP, 0, 0, tiled=True)
    mine, whole_left = lax.optimization_barrier((incoming.reshape(block_size, shared), whole_left))
    gradient = lax.all_gather(mine, "dp", axis=1, tiled=True)
    inner = jnp.einsum(
        "rk,kc->rc",
        gradient,
        right_cols.reshape(block_size, shared),
        preferred_element_type=jnp.float32,
    )
    high = lax.reduce_precision(inner, 8, 7)
    low = (inner - high).astype(jnp.bfloat16)
    high = high.astype(jnp.bfloat16)
    both = jnp.einsum(
        "kr,rc->kc", whole_left, high, preferred_element_type=jnp.float32
    ) + jnp.einsum("kr,rc->kc", whole_left, low, preferred_element_type=jnp.float32)
    partial = split_terms(jnp.sum(both * both))
    lanes = jnp.concatenate([jnp.stack(partial), jnp.zeros(shared - 3, jnp.bfloat16)])
    marks = jnp.broadcast_to(lanes[None, None, :], (total_slots, 8, shared))
    both = both.astype(jnp.bfloat16).reshape(total_slots, row_dev, shared)
    back = lax.all_to_all(jnp.concatenate([both, marks], axis=1), FSDP, 0, 0, tiled=True)
    row_start = lax.axis_index("dp") * shared
    own_rows = lax.dynamic_slice_in_dim(gradient, row_start, shared, 0)
    left_new = left_stats + jnp.einsum(
        "rc,kc->rk", own_rows, gradient, preferred_element_type=jnp.float32
    )
    right_new = right_stats + jnp.einsum(
        "rc,rk->ck", mine, gradient, preferred_element_type=jnp.float32
    )
    picked = jnp.take(back, block_slot, axis=0)
    terms = jnp.zeros((32, shared), jnp.bfloat16).at[:block_count].set(picked[:, row_dev, :])
    tiles = picked[:, :row_dev].reshape(block_count * row_dev, shared)
    gathered = lax.all_gather(jnp.concatenate([tiles, terms]), "dp", axis=0, tiled=False)
    full = gathered[:, : block_count * row_dev].reshape(replicas, block_count, row_dev, shared)
    terms = gathered[:, block_count * row_dev :][:, :block_count, :3].astype(jnp.float32)
    squares = jnp.sum(terms, axis=(0, 2))
    factor = lax.rsqrt(squares / (block_size * block_size) + epsilon)
    update = (full.astype(jnp.float32) * factor[None, :, None, None]).astype(jnp.bfloat16)
    update = update.transpose(2, 1, 0, 3).reshape(row_dev, col_count)
    return (left_new, right_new, update)


def solution(mesh):
    split = Mesh(
        mesh.devices.reshape(4, 8, 2, mesh.shape["dp"]), ("fsdp_0", "fsdp_1", "fsdp_2", "dp")
    )
    placed = (
        P("dp", FSDP, None),
        P(),
        P(FSDP, "dp", None),
        P(FSDP, "dp", None),
        P(FSDP, "dp", None),
        P(FSDP, "dp", None),
    )
    return jax.shard_map(
        per_device,
        mesh=split,
        in_specs=placed,
        out_specs=(P(FSDP, "dp", None), P(FSDP, "dp", None), P(FSDP, None)),
        check_vma=False,
    )
```

profile of v0, /device:TPU:8, one launch (start us, length us, event | category | flops | bytes accessed | tf_op | source)
XLA Modules:
  0.0 203.1 jit_solution(17511728519001342608)
XLA Ops:
  7.2 0.7 all-gather.7.cloned.1.call-update
  7.9 1.1 copy.15
  9.0 0.2 copy.16
  9.2 1.3 copy.19
  10.5 0.4 copy.14
  10.9 1.1 pad_maximum_fusion
  12.0 10.3 %all-to-all-start = ((bf16[8,576,128]{2,1,0:T(8,128)(2,1)}), bf16[8,576,128]{2,1,0:T(8,128)(2,1)S(1)}, u32[]{:S(2)}, u32[]{:S(2)}) async-start(bf16[8,576,128]{2,1,0:T(8,128)(2,1)} %pad_maximum_fusion), calls=%async_computation | async-start | bytes 2359296 | tf_op jit(solution)/shard_map/all_to_all | solution.py:36
  22.4 0.1 select_reduce_fusion
  22.5 0.1 fusion.10
  22.6 42.0 %all-to-all-done = bf16[8,576,128]{2,1,0:T(8,128)(2,1)S(1)} async-done(((bf16[8,576,128]{2,1,0:T(8,128)(2,1)}), bf16[8,576,128]{2,1,0:T(8,128)(2,1)S(1)}, u32[]{:S(2)}, u32[]{:S(2)}) %all-to-all-start) | async-done | bytes 1179680 | tf_op jit(solution)/shard_map/all_to_all | solution.py:36
  64.5 0.1 slice_reduce_fusion
  64.7 0.6 gather_fusion
  65.3 0.2 select_select_fusion
  65.5 22.5 %all_to_all.15 = bf16[64,16,128]{2,1,0:T(8,128)(2,1)} all-to-all(bf16[64,16,128]{2,1,0:T(8,128)(2,1)S(1)} %select_select_fusion), channel_id=1, replica_groups=mesh['fsdp_0'=4,'fsdp_1'=8,'fsdp_2'=2,'dp'=8] {'fsdp_0','fsdp_1','fsdp_2'}, dimensions={0} | all-to-all | bytes 524288 | tf_op jit(solution)/shard_map/all_to_all | solution.py:43
  88.0 42.6 %all-gather.5.cloned.1.call-done = bf16[1024,1024]{1,0:T(8,128)(2,1)} async-done(((bf16[1024,128]{1,0:T(8,128)(2,1)}), bf16[1024,1024]{1,0:T(8,128)(2,1)}) %all-gather.5.cloned.1.call-update) | async-done | bytes 2097168 | tf_op jit(solution)/shard_map/all_gather | solution.py:45
  130.7 2.3 %fusion.14 = f32[1024,128]{1,0:T(8,128)S(1)} fusion(bf16[1024,1024]{1,0:T(8,128)(2,1)} %all-gather.5.cloned.1.call-done, bf16[1024,128]{1,0:T(8,128)(2,1)S(1)} %bitcast.64), kind=kOutput, calls=%fused_computation.42 | convolution fusion | flops 268435456 | bytes 2883584 | tf_op jit(solution)/shard_map/rk,kc->rc/dot_general | solution.py:46
  133.0 0.7 fusion.6
  133.7 0.9 copy-done.2
  134.6 1.3 fusion.13
  140.8 0.1 pad_maximum_fusion.2
  140.9 0.8 pad_maximum_fusion.1
  141.7 10.4 %all-to-all-start.2 = ((bf16[64,24,128]{2,1,0:T(8,128)(2,1)}), bf16[64,24,128]{2,1,0:T(8,128)(2,1)S(1)}, u32[]{:S(2)}, u32[]{:S(2)}) async-start(bf16[64,24,128]{2,1,0:T(8,128)(2,1)} %pad_maximum_fusion.1), calls=%async_computation.2 | async-start | bytes 786432 | tf_op jit(solution)/shard_map/all_to_all | solution.py:62
  152.2 1.6 fusion.1
  153.8 1.3 fusion.2
  155.1 11.5 %all-to-all-done.2 = bf16[64,24,128]{2,1,0:T(8,128)(2,1)S(1)} async-done(((bf16[64,24,128]{2,1,0:T(8,128)(2,1)}), bf16[64,24,128]{2,1,0:T(8,128)(2,1)S(1)}, u32[]{:S(2)}, u32[]{:S(2)}) %all-to-all-start.2) | async-done | bytes 393248 | tf_op jit(solution)/shard_map/all_to_all | solution.py:62
  166.5 0.6 gather_fusion.1
  167.1 0.1 broadcast_select_fusion
  167.3 26.6 %all-gather.1 = bf16[3840,128]{1,0:T(8,128)(2,1)S(1)} all-gather(bf16[480,128]{1,0:T(8,128)(2,1)S(1)} %fusion.9), channel_id=3, replica_groups=mesh['fsdp_0'=4,'fsdp_1'=8,'fsdp_2'=2,'dp'=8] {'dp'}, dimensions={0}, use_global_device_ids=true | all-gather | bytes 1105920 | tf_op jit(solution)/shard_map/all_gather | solution.py:74
  193.9 0.1 convert_reduce_fusion
  194.2 0.3 fusion.3
  194.4 0.6 copy.17
  195.0 1.3 copy.23
  (32 shorter events, 0.3 us)
Async XLA Ops:
  7.2 80.8 %all-gather.7.cloned.1.call-start = ((), (), s32[]{:S(2)}) async-start(), calls=%async_computation.4 | async-start | bytes 2359296 | tf_op jit(solution)/shard_map/all_gather | solution.py:31
  10.9 11.5 %copy-start.6 = (s32[28]{0:T(128)S(1)}, s32[28]{0:T(128)}, u32[]{:S(2)}) copy-start(s32[28]{0:T(128)} %param.9) | copy-start | bytes 340
  12.0 52.5 %all-to-all-start = ((bf16[8,576,128]{2,1,0:T(8,128)(2,1)}), bf16[8,576,128]{2,1,0:T(8,128)(2,1)S(1)}, u32[]{:S(2)}, u32[]{:S(2)}) async-start(bf16[8,576,128]{2,1,0:T(8,128)(2,1)} %pad_maximum_fusion), calls=%async_computation | async-start | bytes 2359296 | tf_op jit(solution)/shard_map/all_to_all | solution.py:36
  22.3 108.3 %all-gather.5.cloned.1.call-start = ((), (), s32[]{:S(2)}) async-start(), calls=%async_computation.3 | async-start | bytes 2359296 | tf_op jit(solution)/shard_map/all_gather | solution.py:45
  88.0 45.0 %copy-start.1 = (bf16[1,1024,1024]{2,1,0:T(8,128)(2,1)S(1)}, bf16[1,1024,1024]{2,1,0:T(8,128)(2,1)}, u32[]{:S(2)}) copy-start(bf16[1,1024,1024]{2,1,0:T(8,128)(2,1)} %all-gather.7.cloned.1.call-done) | copy-start | bytes 6291460
  133.0 1.6 copy-start.2
  134.6 17.6 %copy-start = (bf16[1024,1024]{1,0:T(8,128)(2,1)S(1)}, bf16[1024,1024]{1,0:T(8,128)(2,1)}, u32[]{:S(2)}) copy-start(bf16[1024,1024]{1,0:T(8,128)(2,1)} %all-gather.5.cloned.1.call-done) | copy-start | bytes 6291460
  134.6 17.6 %copy-start.4 = (f32[1,128,1024]{2,1,0:T(8,128)S(1)}, f32[1,128,1024]{2,1,0:T(8,128)}, u32[]{:S(2)}) copy-start(f32[1,128,1024]{2,1,0:T(8,128)} %param.10) | copy-start | bytes 1572868
  141.7 12.1 %copy-start.3 = (bf16[64,16,128]{2,1,0:T(8,128)(2,1)S(1)}, bf16[64,16,128]{2,1,0:T(8,128)(2,1)}, u32[]{:S(2)}) copy-start(bf16[64,16,128]{2,1,0:T(8,128)(2,1)} %all_to_all.15) | copy-start | bytes 786436
  141.7 24.8 %all-to-all-start.2 = ((bf16[64,24,128]{2,1,0:T(8,128)(2,1)}), bf16[64,24,128]{2,1,0:T(8,128)(2,1)S(1)}, u32[]{:S(2)}, u32[]{:S(2)}) async-start(bf16[64,24,128]{2,1,0:T(8,128)(2,1)} %pad_maximum_fusion.1), calls=%async_computation.2 | async-start | bytes 786432 | tf_op jit(solution)/shard_map/all_to_all | solution.py:62
  152.1 1.7 copy-start.5
Sparse Core Ops, SparseCore 0:
  10.1 64.5 all-gather.6
  88.1 42.4 all-gather.4
where the time goes:
time: 204 us; the launch traced here: 203 us
  waiting for transfers between devices  96.7 us (47%)
  blocking collectives  49.1 us (24%)
  starting transfers between devices  20.8 us (10%)
  between operations  19.2 us (9%)
  matrix products  7.21 us (4%)
  local copies, waits for them, and re-layouts  7.09 us (3%)
  other arithmetic  3.03 us (1%)
    all_gather x1, waiting for transfers between devices, per_device(): gradient = lax.all_gather(mine, 'dp', axis=1, tiled=True)  42.6 us
    all_to_all x1, waiting for transfers between devices, per_device(): received = lax.all_to_all(message, 'dp', 0, 0, tiled=True)  42 us
    all_gather x1, blocking collectives, per_device(): lax.all_gather(jnp.concatenate([tiles, terms]), 'dp', axis=0, tiled=False)  26.6 us
    all_to_all x1, blocking collectives, per_device(): incoming = lax.all_to_all(outgoing, FSDP, 0, 0, tiled=True)  22.5 us
    all_to_all x1, waiting for transfers between devices, per_device(): lax.all_to_all(jnp.concatenate([both, marks], axis=1), FSDP, 0, 0, tiled=...  11.5 us
    all_to_all x1, starting transfers between devices, per_device(): lax.all_to_all(jnp.concatenate([both, marks], axis=1), FSDP, 0, 0, tiled=...  10.4 us
    all_to_all x1, starting transfers between devices, per_device(): received = lax.all_to_all(message, 'dp', 0, 0, tiled=True)  10.3 us
    unnamed x18, local copies, waits for them, and re-layouts  4.61 us
  transfers between devices with their start and end apart: 4, of which 3 were waited for; matrix products, arithmetic and copies ran while one was open for 4% of the time, Pallas kernels for 0%

commit v1 on v0

--- a/solution.py
+++ b/solution.py
@@ -6,6 +6,12 @@
 
 FSDP = ("fsdp_0", "fsdp_1", "fsdp_2")
 epsilon = 1e-06
+
+
+def joined_along(blocks, dim):
+    blocks = jnp.moveaxis(blocks, 0, dim)
+    dims = blocks.shape
+    return blocks.reshape(*dims[:dim], dims[dim] * dims[dim + 1], *dims[dim + 2 :])
 
 
 def split_terms(value):
@@ -42,7 +48,19 @@
     )
     incoming = lax.all_to_all(outgoing, FSDP, 0, 0, tiled=True)
     mine, whole_left = lax.optimization_barrier((incoming.reshape(block_size, shared), whole_left))
-    gradient = lax.all_gather(mine, "dp", axis=1, tiled=True)
+    size = lax.axis_size("dp")
+    pairs = [(i, (i + 1) % size) for i in range(size)]
+    back_2 = [(b, a) for a, b in pairs]
+    lower, upper = ([], [])
+    for step in range(size - 1):
+        if step % 2 == 0:
+            lower.append(lax.ppermute(lower[-1] if lower else mine, "dp", pairs))
+        else:
+            upper.append(lax.ppermute(upper[-1] if upper else mine, "dp", back_2))
+    tiles_2 = jnp.stack([*lower[::-1], mine, *upper])
+    shift = lax.axis_index("dp") - len(lower)
+    tiles_2 = tiles_2[(jnp.arange(size) - shift) % size]
+    gradient = joined_along(tiles_2, 1)
     inner = jnp.einsum(
         "rk,kc->rc",
         gradient,

time: 204 us -> 203 us (level)
  waiting for transfers between devices: 96.7 us -> 66.8 us
  starting transfers between devices: 20.8 us -> 39.4 us
  local copies, waits for them, and re-layouts: 7.09 us -> 17 us
    all_gather x1 -> x0, waiting for transfers between devices: 42.6 us -> none  [per_device(): gradient = lax.all_gather(mine, 'dp', axis=1, tiled=True)]
    ppermute x0 -> x7, starting transfers between devices: none -> 23 us  [the longest x3 15.4 us: per_device(): upper.append(lax.ppermute(upper[-1] if upper else mine, 'dp', back_2))]
    ppermute x0 -> x7, waiting for transfers between devices: none -> 18.1 us  [the longest x4 18.1 us: per_device(): lower.append(lax.ppermute(lower[-1] if lower else mine, 'dp', pairs))]
    all_to_all x1, waiting for transfers between devices: 11.5 us -> 7.01 us  [per_device(): lax.all_to_all(jnp.concatenate([both, marks], axis=1), FSDP, 0, 0, tiled=...]
    all_to_all x1, starting transfers between devices: 10.4 us -> 6 us  [per_device(): lax.all_to_all(jnp.concatenate([both, marks], axis=1), FSDP, 0, 0, tiled=...]
    unnamed x18 -> x23, local copies, waits for them, and re-layouts: 4.61 us -> 8.69 us
    gather x0 -> x1, local copies, waits for them, and re-layouts: none -> 2.54 us  [per_device(): tiles_2 = tiles_2[(jnp.arange(size) - shift) % size]]
    transpose x1, local copies, waits for them, and re-layouts: 0.36 us -> 2.62 us  [joined_along(): blocks = jnp.moveaxis(blocks, 0, dim)]
  transfers between devices with their start and end apart: 4 -> 10, of which waited for: 3 -> 6; matrix products, arithmetic and copies ran while one was open for 4% -> 8% of each run, Pallas kernels for 0% -> 0%
where the time goes in v1:
time: 203 us; the launch traced here: 202 us
  waiting for transfers between devices  66.8 us (33%)
  blocking collectives  49 us (24%)
  starting transfers between devices  39.4 us (19%)
  between operations  19.3 us (10%)
  local copies, waits for them, and re-layouts  17 us (8%)
  matrix products  7.46 us (4%)
  other arithmetic  3.04 us (1%)
    all_to_all x1, waiting for transfers between devices, per_device(): received = lax.all_to_all(message, 'dp', 0, 0, tiled=True)  41 us
    all_gather x1, blocking collectives, per_device(): lax.all_gather(jnp.concatenate([tiles, terms]), 'dp', axis=0, tiled=False)  26.6 us
    all_to_all x1, blocking collectives, per_device(): incoming = lax.all_to_all(outgoing, FSDP, 0, 0, tiled=True)  22.3 us
    ppermute x4, waiting for transfers between devices, per_device(): lower.append(lax.ppermute(lower[-1] if lower else mine, 'dp', pairs))  18.1 us
    ppermute x3, starting transfers between devices, per_device(): upper.append(lax.ppermute(upper[-1] if upper else mine, 'dp', back_2))  15.4 us
    all_to_all x1, starting transfers between devices, per_device(): received = lax.all_to_all(message, 'dp', 0, 0, tiled=True)  10.3 us
    unnamed x23, local copies, waits for them, and re-layouts  8.69 us
    ppermute x4, starting transfers between devices, per_device(): lower.append(lax.ppermute(lower[-1] if lower else mine, 'dp', pairs))  7.64 us
  transfers between devices with their start and end apart: 10, of which 6 were waited for; matrix products, arithmetic and copies ran while one was open for 8% of the time, Pallas kernels for 0%

profile of v1, /device:TPU:8, one launch (start us, length us, event | category | flops | bytes accessed | tf_op | source)
XLA Modules:
  0.0 202.0 jit_solution(14382854452556223865)
XLA Ops:
  7.9 1.3 copy.25
  10.0 1.1 pad_maximum_fusion
  11.1 10.3 %all-to-all-start = ((bf16[8,576,128]{2,1,0:T(8,128)(2,1)}), bf16[8,576,128]{2,1,0:T(8,128)(2,1)S(1)}, u32[]{:S(2)}, u32[]{:S(2)}) async-start(bf16[8,576,128]{2,1,0:T(8,128)(2,1)} %pad_maximum_fusion), calls=%async_computation | async-start | bytes 2359296 | tf_op jit(solution)/shard_map/all_to_all | solution.py:42
  21.6 41.0 %all-to-all-done = bf16[8,576,128]{2,1,0:T(8,128)(2,1)S(1)} async-done(((bf16[8,576,128]{2,1,0:T(8,128)(2,1)}), bf16[8,576,128]{2,1,0:T(8,128)(2,1)S(1)}, u32[]{:S(2)}, u32[]{:S(2)}) %all-to-all-start) | async-done | bytes 1179680 | tf_op jit(solution)/shard_map/all_to_all | solution.py:42
  63.5 22.3 %all_to_all.15 = bf16[64,16,128]{2,1,0:T(8,128)(2,1)S(1)} all-to-all(bf16[64,16,128]{2,1,0:T(8,128)(2,1)S(1)} %select_select_fusion), channel_id=1, replica_groups=mesh['fsdp_0'=4,'fsdp_1'=8,'fsdp_2'=2,'dp'=8] {'fsdp_0','fsdp_1','fsdp_2'}, dimensions={0} | all-to-all | bytes 524288 | tf_op jit(solution)/shard_map/all_to_all | solution.py:49
  85.9 1.9 collective-permute-start
  87.8 9.5 %collective-permute-done = bf16[1024,128]{1,0:T(8,128)(2,1)S(1)} collective-permute-done((bf16[1024,128]{1,0:T(8,128)(2,1)S(1)}, bf16[1024,128]{1,0:T(8,128)(2,1)S(1)}, u32[]{:S(2)}, u32[]{:S(2)}) %collective-permute-start) | collective-permute-done | bytes 262176 | tf_op jit(solution)/shard_map/ppermute | solution.py:57
  97.3 1.9 collective-permute-start.1
  99.3 5.1 %collective-permute-start.4 = (bf16[1024,128]{1,0:T(8,128)(2,1)S(1)}, bf16[1024,128]{1,0:T(8,128)(2,1)S(1)}, u32[]{:S(2)}, u32[]{:S(2)}) collective-permute-start(bf16[1024,128]{1,0:T(8,128)(2,1)S(1)} %bitcast.83), channel_id=1, source_target_pairs={{1,0},{2,1},{3,2},{4,3},{5,4},{6,5},{7,6},{0,7},{9,8},{10,9},{11,1... | collective-permute-start | bytes 786440 | tf_op jit(solution)/shard_map/ppermute | solution.py:59
  104.4 3.5 %collective-permute-done.1 = bf16[1024,128]{1,0:T(8,128)(2,1)S(1)} collective-permute-done((bf16[1024,128]{1,0:T(8,128)(2,1)S(1)}, bf16[1024,128]{1,0:T(8,128)(2,1)S(1)}, u32[]{:S(2)}, u32[]{:S(2)}) %collective-permute-start.1) | collective-permute-done | bytes 262176 | tf_op jit(solution)/shard_map/ppermute | solution.py:57
  107.9 1.9 collective-permute-start.2
  109.9 5.1 %collective-permute-start.5 = (bf16[1024,128]{1,0:T(8,128)(2,1)S(1)}, bf16[1024,128]{1,0:T(8,128)(2,1)S(1)}, u32[]{:S(2)}, u32[]{:S(2)}) collective-permute-start(bf16[1024,128]{1,0:T(8,128)(2,1)S(1)} %collective-permute-done.4), channel_id=1, source_target_pairs={{1,0},{2,1},{3,2},{4,3},{5,4},{6,5},{7,6},{0,7},{9,8},{10,9},{11,1... | collective-permute-start | bytes 786440 | tf_op jit(solution)/shard_map/ppermute | solution.py:59
  115.0 2.7 %collective-permute-done.2 = bf16[1024,128]{1,0:T(8,128)(2,1)S(1)} collective-permute-done((bf16[1024,128]{1,0:T(8,128)(2,1)S(1)}, bf16[1024,128]{1,0:T(8,128)(2,1)S(1)}, u32[]{:S(2)}, u32[]{:S(2)}) %collective-permute-start.2) | collective-permute-done | bytes 262176 | tf_op jit(solution)/shard_map/ppermute | solution.py:57
  117.7 1.9 collective-permute-start.3
  119.6 5.1 %collective-permute-start.6 = (bf16[1024,128]{1,0:T(8,128)(2,1)S(1)}, bf16[1024,128]{1,0:T(8,128)(2,1)S(1)}, u32[]{:S(2)}, u32[]{:S(2)}) collective-permute-start(bf16[1024,128]{1,0:T(8,128)(2,1)S(1)} %collective-permute-done.5), channel_id=1, source_target_pairs={{1,0},{2,1},{3,2},{4,3},{5,4},{6,5},{7,6},{0,7},{9,8},{10,9},{11,1... | collective-permute-start | bytes 786440 | tf_op jit(solution)/shard_map/ppermute | solution.py:59
  124.8 2.4 %collective-permute-done.3 = bf16[1024,128]{1,0:T(8,128)(2,1)S(1)} collective-permute-done((bf16[1024,128]{1,0:T(8,128)(2,1)S(1)}, bf16[1024,128]{1,0:T(8,128)(2,1)S(1)}, u32[]{:S(2)}, u32[]{:S(2)}) %collective-permute-start.3) | collective-permute-done | bytes 262176 | tf_op jit(solution)/shard_map/ppermute | solution.py:57
  127.9 0.7 bitcast_dynamic-update-slice_fusion.6
  128.6 0.7 bitcast_dynamic-update-slice_fusion.5
  129.3 0.7 bitcast_dynamic-update-slice_fusion.4
  130.1 0.7 bitcast_dynamic-update-slice_fusion.3
  131.5 0.7 bitcast_dynamic-update-slice_fusion.1
  132.9 2.5 %gather_fusion.1 = bf16[8,1024,128]{2,1,0:T(8,128)(2,1)S(1)} fusion(bf16[8,1024,128]{2,1,0:T(8,128)(2,1)} %bitcast_dynamic-update-slice_fusion, s32[1024]{0:T(1024)S(1)} %pad_clamp_fusion.1), kind=kCustom, calls=%fused_computation.1 | custom fusion | bytes 4194336 | tf_op jit(solution)/shard_map/gather | solution.py:62
  136.2 0.9 copy-done.1
  137.8 1.3 fusion.17
  144.1 0.8 pad_maximum_fusion.1
  144.9 6.0 %all-to-all-start.2 = ((bf16[64,24,128]{2,1,0:T(8,128)(2,1)}), bf16[64,24,128]{2,1,0:T(8,128)(2,1)S(1)}, u32[]{:S(2)}, u32[]{:S(2)}) async-start(bf16[64,24,128]{2,1,0:T(8,128)(2,1)} %pad_maximum_fusion.1), calls=%async_computation.2 | async-start | bytes 786432 | tf_op jit(solution)/shard_map/all_to_all | solution.py:80
  151.0 2.6 %copy.22 = bf16[1024,8,128]{0,2,1:T(8,128)(2,1)} copy(bf16[1024,8,128]{2,0,1:T(8,128)(2,1)S(1)} %bitcast.71) | data formatting | bytes 4194304 | tf_op jit(solution)/shard_map/transpose | solution.py:12
  153.6 3.1 %fusion.1 = f32[1,128,1024]{2,1,0:T(8,128)} fusion(f32[1,128,1024]{2,1,0:T(8,128)S(1)} %copy-done.2, bf16[1024,1024]{0,1:T(8,128)(2,1)} %bitcast.72, s32[]{:T(128)S(6)} %select_n.71), kind=kOutput, calls=%fused_computation.9 | convolution fusion | flops 268566528 | bytes 3407876 | tf_op jit(solution)/shard_map/rc,kc->rk/dot_general | solution.py:83
  156.7 1.6 fusion.2
  158.3 7.0 %all-to-all-done.2 = bf16[64,24,128]{2,1,0:T(8,128)(2,1)S(1)} async-done(((bf16[64,24,128]{2,1,0:T(8,128)(2,1)}), bf16[64,24,128]{2,1,0:T(8,128)(2,1)S(1)}, u32[]{:S(2)}, u32[]{:S(2)}) %all-to-all-start.2) | async-done | bytes 393248 | tf_op jit(solution)/shard_map/all_to_all | solution.py:80
  166.1 26.6 %all-gather.1 = bf16[3840,128]{1,0:T(8,128)(2,1)S(1)} all-gather(bf16[480,128]{1,0:T(8,128)(2,1)S(1)} %fusion.10), channel_id=3, replica_groups=mesh['fsdp_0'=4,'fsdp_1'=8,'fsdp_2'=2,'dp'=8] {'dp'}, dimensions={0}, use_global_device_ids=true | all-gather | bytes 1105920 | tf_op jit(solution)/shard_map/all_gather | solution.py:92
  193.8 1.3 copy.29
  (52 shorter events, 8.1 us)
Async XLA Ops:
  7.2 2.4 %copy-start.4 = (bf16[1,128,1024]{2,1,0:T(8,128)(2,1)S(1)}, bf16[1,128,1024]{2,1,0:T(8,128)(2,1)}, u32[]{:S(2)}) copy-start(bf16[1,128,1024]{2,1,0:T(8,128)(2,1)} %param.13) | copy-start | bytes 786436
  7.2 78.7 %all-gather.4.cloned.1.call-start = ((), (), s32[]{:S(2)}) async-start(), calls=%async_computation.3 | async-start | bytes 2359296 | tf_op jit(solution)/shard_map/all_gather | solution.py:37
  9.9 11.4 %copy-start.5 = (s32[28]{0:T(128)S(1)}, s32[28]{0:T(128)}, u32[]{:S(2)}) copy-start(s32[28]{0:T(128)} %param.9) | copy-start | bytes 340
  11.1 51.5 %all-to-all-start = ((bf16[8,576,128]{2,1,0:T(8,128)(2,1)}), bf16[8,576,128]{2,1,0:T(8,128)(2,1)S(1)}, u32[]{:S(2)}, u32[]{:S(2)}) async-start(bf16[8,576,128]{2,1,0:T(8,128)(2,1)} %pad_maximum_fusion), calls=%async_computation | async-start | bytes 2359296 | tf_op jit(solution)/shard_map/all_to_all | solution.py:42
  85.9 11.5 %collective-permute-start = (bf16[1024,128]{1,0:T(8,128)(2,1)S(1)}, bf16[1024,128]{1,0:T(8,128)(2,1)S(1)}, u32[]{:S(2)}, u32[]{:S(2)}) collective-permute-start(bf16[1024,128]{1,0:T(8,128)(2,1)S(1)} %bitcast.82), channel_id=1, source_target_pairs={{0,1},{1,2},{2,3},{3,4},{4,5},{5,6},{6,7},{7,0},{8,9},{9,10},{10,1... | collective-permute-start | bytes 786440 | tf_op jit(solution)/shard_map/ppermute | solution.py:57
  97.3 10.6 %collective-permute-start.1 = (bf16[1024,128]{1,0:T(8,128)(2,1)S(1)}, bf16[1024,128]{1,0:T(8,128)(2,1)S(1)}, u32[]{:S(2)}, u32[]{:S(2)}) collective-permute-start(bf16[1024,128]{1,0:T(8,128)(2,1)S(1)} %collective-permute-done), channel_id=1, source_target_pairs={{0,1},{1,2},{2,3},{3,4},{4,5},{5,6},{6,7},{7,0},{8,9},{9,10},{10,1... | collective-permute-start | bytes 786440 | tf_op jit(solution)/shard_map/ppermute | solution.py:57
  99.3 10.6 %collective-permute-start.4 = (bf16[1024,128]{1,0:T(8,128)(2,1)S(1)}, bf16[1024,128]{1,0:T(8,128)(2,1)S(1)}, u32[]{:S(2)}, u32[]{:S(2)}) collective-permute-start(bf16[1024,128]{1,0:T(8,128)(2,1)S(1)} %bitcast.83), channel_id=1, source_target_pairs={{1,0},{2,1},{3,2},{4,3},{5,4},{6,5},{7,6},{0,7},{9,8},{10,9},{11,1... | collective-permute-start | bytes 786440 | tf_op jit(solution)/shard_map/ppermute | solution.py:59
  107.9 9.8 %collective-permute-start.2 = (bf16[1024,128]{1,0:T(8,128)(2,1)S(1)}, bf16[1024,128]{1,0:T(8,128)(2,1)S(1)}, u32[]{:S(2)}, u32[]{:S(2)}) collective-permute-start(bf16[1024,128]{1,0:T(8,128)(2,1)S(1)} %collective-permute-done.1), channel_id=1, source_target_pairs={{0,1},{1,2},{2,3},{3,4},{4,5},{5,6},{6,7},{7,0},{8,9},{9,10},{10,1... | collective-permute-start | bytes 786440 | tf_op jit(solution)/shard_map/ppermute | solution.py:57
  109.9 9.7 %collective-permute-start.5 = (bf16[1024,128]{1,0:T(8,128)(2,1)S(1)}, bf16[1024,128]{1,0:T(8,128)(2,1)S(1)}, u32[]{:S(2)}, u32[]{:S(2)}) collective-permute-start(bf16[1024,128]{1,0:T(8,128)(2,1)S(1)} %collective-permute-done.4), channel_id=1, source_target_pairs={{1,0},{2,1},{3,2},{4,3},{5,4},{6,5},{7,6},{0,7},{9,8},{10,9},{11,1... | collective-permute-start | bytes 786440 | tf_op jit(solution)/shard_map/ppermute | solution.py:59
  117.7 9.5 %collective-permute-start.3 = (bf16[1024,128]{1,0:T(8,128)(2,1)S(1)}, bf16[1024,128]{1,0:T(8,128)(2,1)S(1)}, u32[]{:S(2)}, u32[]{:S(2)}) collective-permute-start(bf16[1024,128]{1,0:T(8,128)(2,1)S(1)} %collective-permute-done.2), channel_id=1, source_target_pairs={{0,1},{1,2},{2,3},{3,4},{4,5},{5,6},{6,7},{7,0},{8,9},{9,10},{10,1... | collective-permute-start | bytes 786440 | tf_op jit(solution)/shard_map/ppermute | solution.py:57
  119.6 12.6 %collective-permute-start.6 = (bf16[1024,128]{1,0:T(8,128)(2,1)S(1)}, bf16[1024,128]{1,0:T(8,128)(2,1)S(1)}, u32[]{:S(2)}, u32[]{:S(2)}) collective-permute-start(bf16[1024,128]{1,0:T(8,128)(2,1)S(1)} %collective-permute-done.5), channel_id=1, source_target_pairs={{1,0},{2,1},{3,2},{4,3},{5,4},{6,5},{7,6},{0,7},{9,8},{10,9},{11,1... | collective-permute-start | bytes 786440 | tf_op jit(solution)/shard_map/ppermute | solution.py:59
  135.5 1.6 copy-start.1
  144.9 20.4 %all-to-all-start.2 = ((bf16[64,24,128]{2,1,0:T(8,128)(2,1)}), bf16[64,24,128]{2,1,0:T(8,128)(2,1)S(1)}, u32[]{:S(2)}, u32[]{:S(2)}) async-start(bf16[64,24,128]{2,1,0:T(8,128)(2,1)} %pad_maximum_fusion.1), calls=%async_computation.2 | async-start | bytes 786432 | tf_op jit(solution)/shard_map/all_to_all | solution.py:80
  150.9 2.6 %copy-start.2 = (f32[1,128,1024]{2,1,0:T(8,128)S(1)}, f32[1,128,1024]{2,1,0:T(8,128)}, u32[]{:S(2)}) copy-start(f32[1,128,1024]{2,1,0:T(8,128)} %param.10) | copy-start | bytes 1572868
  153.6 3.1 %copy-start = (bf16[1024,8,128]{0,2,1:T(8,128)(2,1)S(1)}, bf16[1024,8,128]{0,2,1:T(8,128)(2,1)}, u32[]{:S(2)}) copy-start(bf16[1024,8,128]{0,2,1:T(8,128)(2,1)} %copy.22) | copy-start | bytes 6291460
  153.6 3.1 %copy-start.3 = (f32[1,128,1024]{2,1,0:T(8,128)S(1)}, f32[1,128,1024]{2,1,0:T(8,128)}, u32[]{:S(2)}) copy-start(f32[1,128,1024]{2,1,0:T(8,128)} %param.11) | copy-start | bytes 1572868
Sparse Core Ops, SparseCore 0:
  10.1 63.5 all-gather.3
